TPU v7x, 32 devices: a 4x4x1 block of a 4x4x8 slice. The times are simulated.
32 devices in a mesh: dp: 2 (over z, core), tp: 16 (over x, y).
Axes of the slice: x: 4, y: 4, z: 1, core: 2. Of those that a mesh axis runs over, the one named last changes fastest.
The devices are a block of a 4x4x8 slice.
Arguments:
- x: bfloat16 [4096, 7168], P('dp'), parts along dimension 0
- w_gate: bfloat16 [7168, 20480], P(None, 'tp')
- w_up: bfloat16 [7168, 20480], P(None, 'tp')
- w_down: bfloat16 [20480, 7168], P('tp')
Outputs:
- output: bfloat16 [4096, 7168], P('dp'), parts along dimension 0
There are 2 independent parts. A program takes and returns all parts, laid end to end along the dimension named above; an argument that names none is the same for every part.
All inputs are finite; a program needn't handle non-finite values.
Results may differ from a plain program's by a relative error of at most 0.016.
Values are sent between devices in bfloat16 or wider.
A program may use at most 768 MiB of HBM per device.

v0:
```python
import jax
import jax.numpy as jnp
from jax import lax
from jax.sharding import PartitionSpec as P


def solution(mesh):
    def step(x, w_gate, w_up, w_down):
        gate = jnp.dot(x, w_gate, preferred_element_type=jnp.float32)
        up = jnp.dot(x, w_up, preferred_element_type=jnp.float32)
        hidden = (jax.nn.silu(gate) * up).astype(jnp.bfloat16)
        term = jnp.dot(hidden, w_down, preferred_element_type=jnp.float32).astype(jnp.bfloat16)
        return lax.psum(term, "tp")

    return jax.shard_map(
        step,
        mesh=mesh,
        in_specs=(P("dp", None), P(None, "tp"), P(None, "tp"), P("tp", None)),
        out_specs=P("dp", None),
        check_vma=False,
    )
```

profile of v0, /device:TPU:97, one launch (start us, length us, event | category | flops | bytes accessed | tf_op | source)
XLA Modules:
  0.0 515.6 jit_solution(3297667925035416627)
XLA Ops:
  6.5 0.0 all-reduce.2.cloned.1.call-start
  6.6 46.7 %fusion.1 = f32[2048,1280]{1,0:T(8,128)} fusion(bf16[2048,7168]{1,0:T(8,128)(2,1)} %param.4, bf16[7168,1280]{1,0:T(8,128)(2,1)} %param.5), kind=kOutput, calls=%fused_computation.3 | convolution fusion | flops 37580963840 | bytes 58195968 | tf_op jit(solution)/shard_map/dot_general | solution.py:9
  53.3 48.1 %fusion = bf16[2048,1280]{1,0:T(8,128)(2,1)S(1)} fusion(bf16[2048,7168]{1,0:T(8,128)(2,1)} %param.4, bf16[7168,1280]{1,0:T(8,128)(2,1)} %param.6, f32[2048,1280]{1,0:T(8,128)} %fusion.1), kind=kOutput, calls=%fused_computation.2 | convolution fusion | flops 37596692480 | bytes 63438848 | tf_op jit(solution)/shard_map/dot_general | solution.py:10
  101.4 46.9 %convolution_convert_fusion = bf16[2048,7168]{1,0:T(8,128)(2,1)} fusion(bf16[2048,1280]{1,0:T(8,128)(2,1)S(1)} %fusion, bf16[1280,7168]{1,0:T(8,128)(2,1)} %param.7), kind=kOutput, calls=%fused_computation | convolution fusion | flops 37595643904 | bytes 52953088 | tf_op jit(solution)/shard_map/dot_general | solution.py:12
  148.2 0.1 all-reduce.2.cloned.1.call-update
  148.3 340.3 %all-reduce.2.cloned.1.call-done = bf16[2048,7168]{1,0:T(8,128)(2,1)} async-done(((bf16[2048,7168]{1,0:T(8,128)(2,1)}), bf16[2048,7168]{1,0:T(8,128)(2,1)}) %all-reduce.2.cloned.1.call-update) | async-done | bytes 29360144 | tf_op jit(solution)/shard_map/psum | solution.py:13
  488.6 20.1 %copy.6 = bf16[2048,7168]{1,0:T(8,128)(2,1)} copy(bf16[2048,7168]{1,0:T(8,128)(2,1)} %all-reduce.2.cloned.1.call-done) | data formatting | bytes 58720256
Async XLA Ops:
  6.5 482.1 %all-reduce.2.cloned.1.call-start = ((), (), s32[]{:S(2)}) async-start(), calls=%async_computation | async-start | bytes 58720256 | tf_op jit(solution)/shard_map/psum | solution.py:13
Sparse Core Ops, SparseCore 0:
  148.4 340.1 all-reduce.1
where the time goes:
time: 516 us
  waiting for transfers between devices  340 us (66%)
  matrix products  142 us (28%)
  local copies, waits for them, and re-layouts  20.1 us (4%)
  between operations  13.4 us (3%)
    psum x1, waiting for transfers between devices, step(): return lax.psum(term, 'tp')  340 us
    dot_general x1, matrix products, step(): up = jnp.dot(x, w_up, preferred_element_type=jnp.float32)  48.1 us
    dot_general x1, matrix products, step(): jnp.dot(hidden, w_down, preferred_element_type=jnp.float32)  46.9 us
    dot_general x1, matrix products, step(): gate = jnp.dot(x, w_gate, preferred_element_type=jnp.float32)  46.7 us
    unnamed x1, local copies, waits for them, and re-layouts  20.1 us
  transfers between devices with their start and end apart: 1, of which 1 were waited for; matrix products, arithmetic and copies ran while one was open for 0% of the time, Pallas kernels for 0%

commit v1 on v0

v1 whole, which is shorter than its diff:
```python
import functools
import math

import jax
import jax.numpy as jnp
from jax import lax
from jax.experimental import pallas as pl
from jax.experimental.pallas import tpu as pltpu
from jax.sharding import PartitionSpec as P

MESH = pl.DeviceIdType.MESH
COLOURS = 4
CHUNK = 256
TILE = 256
R1, R2, R3, Q1, Q2, Q3, G1, G2, G3, H1, H2, H3 = range(12)


def kernel(cfg, x_hbm, wg_hbm, wu_hbm, wd_hbm, y_hbm,
           xb, wgb, wub, wdb, hb, term, r1, r2, r3, c3, run, s1, s2, q1, q2, q3, cq, fin,
           x_sem, wg_sem, wu_sem, wd_sem, own_sem, send_sem, recv_sem, credit):
    side, chunks, m, q, tiles, tile = cfg
    block, sub = m // side, m // (side * side)
    me = lax.axis_index("tp")
    px, py = me // side, me % side

    def dev(index):
        return {"tp": index}

    def place(k):
        ax = k // 2
        sign = 1 - 2 * (k % 2)
        p1, p2 = px * (1 - ax) + py * ax, py * (1 - ax) + px * ax
        return p1, p2, side * (1 - ax) + ax, (1 - ax) + side * ax, sign

    def step_on(p, stride, delta):
        return me + ((p + delta + side) % side - p) * stride

    def wrap(p, delta):
        return (p + delta + side) % side

    neighbours = [step_on(px, side, 1), step_on(px, side, -1), step_on(py, 1, 1), step_on(py, 1, -1)]
    barrier = pltpu.get_barrier_semaphore()
    for other in neighbours:
        pl.semaphore_signal(barrier, inc=1, device_id=dev(other), device_id_type=MESH)
    pl.semaphore_wait(barrier, len(neighbours))

    def remote(kind, c, k, src, dst, to):
        return pltpu.make_async_remote_copy(
            src_ref=src, dst_ref=dst, send_sem=send_sem.at[kind, c % 2, k],
            recv_sem=recv_sem.at[kind, c % 2, k], device_id=dev(to), device_id_type=MESH)

    def rows_of(start, count):
        return pl.ds(pl.multiple_of(start, count), count)

    def y_at(c, k, p1, p2, count):
        return y_hbm.at[rows_of(c * m + p1 * block + p2 * sub, count), pl.ds(pl.multiple_of(k * q, 128), q)]

    def message(kind, c, k):
        p1, p2, st1, st2, s = place(k)
        par = c % 2
        plus1, minus1 = step_on(p1, st1, s), step_on(p1, st1, -s)
        plus2, minus2 = step_on(p2, st2, s), step_on(p2, st2, -s)
        if kind == R1:
            return remote(kind, c, k, term.at[par, k, rows_of(wrap(p1, 2) * block, block)], r1.at[par, k], minus1)
        if kind == R2:
            return remote(kind, c, k, term.at[par, k, rows_of(wrap(p1, s) * block, block)], r2.at[par, k], plus1)
        if kind == R3:
            return remote(kind, c, k, c3.at[par, k], r3.at[par, k], minus1)
        if kind == Q1:
            return remote(kind, c, k, s1.at[par, k], q1.at[par, k], minus2)
        if kind == Q2:
            return remote(kind, c, k, s2.at[par, k], q2.at[par, k], plus2)
        if kind == Q3:
            return remote(kind, c, k, cq.at[par, k], q3.at[par, k], minus2)
        if kind == G1:
            return remote(kind, c, k, fin.at[par, k], y_at(c, k, p1, p2, sub), plus2)
        if kind == G2:
            return remote(kind, c, k, fin.at[par, k], y_at(c, k, p1, p2, sub), minus2)
        if kind == G3:
            at = y_at(c, k, p1, wrap(p2, -s), sub)
            return remote(kind, c, k, at, at, plus2)
        if kind == H1:
            at = y_at(c, k, p1, 0, block)
            return remote(kind, c, k, at, at, plus1)
        if kind == H2:
            at = y_at(c, k, p1, 0, block)
            return remote(kind, c, k, at, at, minus1)
        at = y_at(c, k, wrap(p1, -s), 0, block)
        return remote(kind, c, k, at, at, plus1)

    def arrived(kind, c, k):
        p1, p2, _, _, s = place(k)
        par = c % 2
        dst = {
            R1: lambda: r1.at[par, k], R2: lambda: r2.at[par, k], R3: lambda: r3.at[par, k],
            Q1: lambda: q1.at[par, k], Q2: lambda: q2.at[par, k], Q3: lambda: q3.at[par, k],
            G1: lambda: y_at(c, k, p1, wrap(p2, -s), sub),
            G2: lambda: y_at(c, k, p1, wrap(p2, s), sub),
            G3: lambda: y_at(c, k, p1, wrap(p2, 2), sub),
            H1: lambda: y_at(c, k, wrap(p1, -s), 0, block),
            H2: lambda: y_at(c, k, wrap(p1, s), 0, block),
            H3: lambda: y_at(c, k, wrap(p1, 2), 0, block),
        }[kind]()
        pltpu.make_async_copy(dst, dst, recv_sem.at[kind, c % 2, k]).wait()

    def own_copy(c, k):
        p1, p2, _, _, _ = place(k)
        return pltpu.make_async_copy(fin.at[c % 2, k], y_at(c, k, p1, p2, sub), own_sem.at[c % 2, k])

    def colours(body):
        def one(k, carry):
            body(k, *place(k))
            return carry
        lax.fori_loop(0, COLOURS, one, 0)

    def by_rows(body):
        def one(i, carry):
            body(pl.multiple_of(i * sub, sub))
            return carry
        lax.fori_loop(0, side, one, 0)

    f32 = jnp.float32

    def stage1(c):
        par, sl = c % 2, c % 3

        def body(k, p1, p2, st1, st2, s):
            message(R1, c, k).wait_send()
            message(R2, c, k).wait_send()
            arrived(R1, c, k)

            def add(i):
                at = pl.ds(i, sub)
                t = term[par, k, pl.ds(pl.multiple_of(wrap(p1, -s) * block + i, sub), sub), :]
                c3[par, k, at, :] = (t.astype(f32) + r1[par, k, at, :].astype(f32)).astype(jnp.bfloat16)
            by_rows(add)
            message(R3, c, k).start()
            arrived(R2, c, k)

            def keep(i):
                at = pl.ds(i, sub)
                t = term[par, k, pl.ds(pl.multiple_of(p1 * block + i, sub), sub), :]
                run[sl, k, at, :] = t.astype(f32) + r2[par, k, at, :].astype(f32)
            by_rows(keep)
        colours(body)

    def stage2(c):
        par, sl = c % 2, c % 3

        def body(k, p1, p2, st1, st2, s):
            message(R3, c, k).wait_send()
            arrived(R3, c, k)

            def add(i):
                at = pl.ds(i, sub)
                run[sl, k, at, :] = run[sl, k, at, :] + r3[par, k, at, :].astype(f32)
            by_rows(add)
            s1[par, k] = run[sl, k, rows_of(wrap(p2, 2) * sub, sub), :].astype(jnp.bfloat16)
            s2[par, k] = run[sl, k, rows_of(wrap(p2, s) * sub, sub), :].astype(jnp.bfloat16)
            message(Q1, c, k).start()
            message(Q2, c, k).start()
        colours(body)

    def stage3(c):
        par, sl = c % 2, c % 3

        def body(k, p1, p2, st1, st2, s):
            message(Q1, c, k).wait_send()
            message(Q2, c, k).wait_send()
            arrived(Q1, c, k)
            there = run[sl, k, rows_of(wrap(p2, -s) * sub, sub), :]
            cq[par, k] = (there + q1[par, k].astype(f32)).astype(jnp.bfloat16)
            message(Q3, c, k).start()
            arrived(Q2, c, k)
            mine = rows_of(p2 * sub, sub)
            run[sl, k, mine, :] = run[sl, k, mine, :] + q2[par, k].astype(f32)
        colours(body)

    def stage4(c):
        par, sl = c % 2, c % 3

        def body(k, p1, p2, st1, st2, s):
            message(Q3, c, k).wait_send()
            arrived(Q3, c, k)
            mine = rows_of(p2 * sub, sub)
            fin[par, k] = (run[sl, k, mine, :] + q3[par, k].astype(f32)).astype(jnp.bfloat16)
            message(G1, c, k).start()
            message(G2, c, k).start()
            own_copy(c, k).start()
        colours(body)

    def stage5(c):
        def body(k, *_):
            message(G1, c, k).wait_send()
            message(G2, c, k).wait_send()
            own_copy(c, k).wait()
            arrived(G1, c, k)
            message(G3, c, k).start()
            arrived(G2, c, k)
        colours(body)

    def stage6(c):
        def body(k, *_):
            message(G3, c, k).wait_send()
            arrived(G3, c, k)
            message(H1, c, k).start()
            message(H2, c, k).start()
        colours(body)

    def stage7(c):
        def body(k, *_):
            message(H1, c, k).wait_send()
            message(H2, c, k).wait_send()
            arrived(H1, c, k)
            message(H3, c, k).start()
            arrived(H2, c, k)
        colours(body)

    def stage8(c):
        def body(k, *_):
            message(H3, c, k).wait_send()
            arrived(H3, c, k)
        colours(body)

    def x_copy(t):
        return pltpu.make_async_copy(x_hbm.at[rows_of(t * m, m), :], xb, x_sem)

    def w_copies(g):
        at = pl.ds(pl.multiple_of((g % tiles) * tile, tile), tile)
        slot = g % 2
        return (pltpu.make_async_copy(wg_hbm.at[:, at], wgb.at[slot], wg_sem.at[slot]),
                pltpu.make_async_copy(wu_hbm.at[:, at], wub.at[slot], wu_sem.at[slot]))

    def colour_at(j):
        return (j % 2) * 2 + j // 2

    def d_copy(j):
        at = pl.ds(pl.multiple_of(colour_at(j) * q, 128), q)
        return pltpu.make_async_copy(wd_hbm.at[:, at], wdb.at[j % 2], wd_sem.at[j % 2])

    x_copy(0).start()
    for g in range(2):
        for copy in w_copies(g):
            copy.start()
    for j in range(2):
        d_copy(j).start()

    def hidden(t):
        x_copy(t).wait()

        def one(n, carry):
            g = t * tiles + n
            slot = g % 2
            for copy in w_copies(g):
                copy.wait()
            gate = jnp.dot(xb[...], wgb[slot], preferred_element_type=f32)
            up = jnp.dot(xb[...], wub[slot], preferred_element_type=f32)
            at = pl.ds(pl.multiple_of(n * tile, tile), tile)
            hb[:, at] = (gate * jax.nn.sigmoid(gate) * up).astype(jnp.bfloat16)

            @pl.when(g + 2 < chunks * tiles)
            def _():
                for copy in w_copies(g + 2):
                    copy.start()
            return carry
        lax.fori_loop(0, tiles, one, 0)

        @pl.when(t + 1 < chunks)
        def _():
            x_copy(t + 1).start()

    def down(t):
        def one(j, carry):
            k = colour_at(j)
            d_copy(j).wait()
            term[t % 2, k] = jnp.dot(hb[...], wdb[j % 2], preferred_element_type=f32).astype(jnp.bfloat16)

            @pl.when((j + 2 < COLOURS) | (t + 1 < chunks))
            def _():
                d_copy((j + 2) % COLOURS).start()
            message(R1, t, k).start()
            message(R2, t, k).start()
            return carry
        lax.fori_loop(0, COLOURS, one, 0)

    late = (stage8, stage7, stage6, stage5, stage4, stage3, stage2)
    steps = chunks + 8

    def step(t, carry):
        @pl.when(t > 0)
        def _():
            for d in range(len(neighbours)):
                pl.semaphore_wait(credit.at[d], 1)

        for i, stage in enumerate(late):
            lag = 8 - i

            @pl.when((t >= lag) & (t < chunks + lag))
            def _(stage=stage, lag=lag):
                stage(t - lag)

        @pl.when(t < chunks)
        def _():
            hidden(t)

        @pl.when((t >= 1) & (t < chunks + 1))
        def _():
            stage1(t - 1)

        @pl.when(t < steps - 1)
        def _():
            for d, other in enumerate(neighbours):
                pl.semaphore_signal(credit.at[d], inc=1, device_id=dev(other), device_id_type=MESH)

        @pl.when(t < chunks)
        def _():
            down(t)
        return carry

    lax.fori_loop(0, steps, step, 0)


def solution(mesh):
    side = math.isqrt(mesh.shape["tp"])
    assert side == 4 and side * side == mesh.shape["tp"]

    def body(x, w_gate, w_up, w_down):
        rows, d = x.shape
        ff = w_gate.shape[1]
        m, q, tile = CHUNK, d // COLOURS, TILE
        chunks, tiles = rows // m, ff // tile
        block, sub = m // side, m // (side * side)
        bf16 = jnp.bfloat16
        any_spec = pl.BlockSpec(memory_space=pl.ANY)
        dma = pltpu.SemaphoreType.DMA
        big = pltpu.VMEM((2, COLOURS, block, q), bf16)
        small = pltpu.VMEM((2, COLOURS, sub, q), bf16)
        return pl.pallas_call(
            functools.partial(kernel, (side, chunks, m, q, tiles, tile)),
            out_shape=jax.ShapeDtypeStruct((rows, d), bf16),
            in_specs=[any_spec] * 4,
            out_specs=any_spec,
            scratch_shapes=[
                pltpu.VMEM((m, d), bf16),
                pltpu.VMEM((2, d, tile), bf16), pltpu.VMEM((2, d, tile), bf16),
                pltpu.VMEM((2, ff, q), bf16),
                pltpu.VMEM((m, ff), bf16),
                pltpu.VMEM((2, COLOURS, m, q), bf16),
                big, big, big, big,
                pltpu.VMEM((3, COLOURS, block, q), jnp.float32),
                small, small, small, small, small, small, small,
                dma, dma((2,)), dma((2,)), dma((2,)), dma((2, COLOURS)),
                dma((12, 2, COLOURS)), dma((12, 2, COLOURS)),
                pltpu.SemaphoreType.REGULAR((4,)),
            ],
            compiler_params=pltpu.CompilerParams(
                collective_id=0, has_side_effects=True, vmem_limit_bytes=66_000_000),
        )(x, w_gate, w_up, w_down)

    return jax.shard_map(
        body,
        mesh=mesh,
        in_specs=(P("dp", None), P(None, "tp"), P(None, "tp"), P("tp", None)),
        out_specs=P("dp", None),
        check_vma=False,
    )
```

time: 516 us -> 364 us (0.71)
  Pallas kernels: 0 us -> 343 us
  waiting for transfers between devices: 340 us -> 0 us
  matrix products: 142 us -> 0 us
  between operations: 13.4 us -> 0.01 us
    pallas_call x0 -> x1, Pallas kernels: none -> 343 us  [body(): pl.pallas_call(functools.partial(kernel, (side, chunks, m, q, tiles, tile...]
    psum x1 -> x0, waiting for transfers between devices: 340 us -> none  [step(): return lax.psum(term, 'tp')]
    dot_general x3 -> x0, matrix products: 142 us -> none  [the longest x1 48.1 us: step(): up = jnp.dot(x, w_up, preferred_element_type=jnp.float32)]
  transfers between devices with their start and end apart: 1 -> 0, of which waited for: 1 -> 0; matrix products, arithmetic and copies ran while one was open for 0% -> 0% of each run, Pallas kernels for 0% -> 0%
where the time goes in v1:
time: 364 us; the launch traced here: 363 us
  Pallas kernels  343 us (94%)
  local copies, waits for them, and re-layouts  20.2 us (6%)
    pallas_call x1, Pallas kernels, body(): pl.pallas_call(functools.partial(kernel, (side, chunks, m, q, tiles, tile...  343 us
    unnamed x1, local copies, waits for them, and re-layouts  20.2 us

profile of v1, /device:TPU:97, one launch (start us, length us, event | category | flops | bytes accessed | tf_op | source)
XLA Modules:
  0.0 362.8 jit_solution(2360637828438600348)
XLA Ops:
  0.0 342.7 %shard_map.46 = bf16[2048,7168]{1,0:T(8,128)(2,1)} custom-call(bf16[2048,7168]{1,0:T(8,128)(2,1)} %x_hbm.1, bf16[7168,1280]{1,0:T(8,128)(2,1)} %wg_hbm.1, bf16[7168,1280]{1,0:T(8,128)(2,1)} %wu_hbm.1, bf16[1280,7168]{1,0:T(8,128)(2,1)} %wd_hbm.1), custom_call_target="tpu_custom_call" | custom-call | tf_op jit(solution)/shard_map/pallas_call | solution.py:338
  342.7 20.2 %copy.6 = bf16[2048,7168]{1,0:T(8,128)(2,1)} copy(bf16[2048,7168]{1,0:T(8,128)(2,1)} %shard_map.46) | data formatting | bytes 58720256

commit v2 on v1

--- a/solution.py
+++ b/solution.py
@@ -12,11 +12,12 @@
 COLOURS = 4
 CHUNK = 256
 TILE = 256
+SLOTS = 3
 R1, R2, R3, Q1, Q2, Q3, G1, G2, G3, H1, H2, H3 = range(12)
 
 
 def kernel(cfg, x_hbm, wg_hbm, wu_hbm, wd_hbm, y_hbm,
-           xb, wgb, wub, wdb, hb, term, r1, r2, r3, c3, run, s1, s2, q1, q2, q3, cq, fin,
+           xb, wb, wdb, hb, term, r1, r2, r3, c3, run, s1, s2, q1, q2, q3, cq, fin,
            x_sem, wg_sem, wu_sem, wd_sem, own_sem, send_sem, recv_sem, credit):
     side, chunks, m, q, tiles, tile = cfg
     block, sub = m // side, m // (side * side)
@@ -122,11 +123,10 @@
     f32 = jnp.float32
 
     def stage1(c):
-        par, sl = c % 2, c % 3
-
-        def body(k, p1, p2, st1, st2, s):
+        par = c % 2
+
+        def pass_on(k, p1, p2, st1, st2, s):
             message(R1, c, k).wait_send()
-            message(R2, c, k).wait_send()
             arrived(R1, c, k)
 
             def add(i):
@@ -135,17 +135,21 @@
                 c3[par, k, at, :] = (t.astype(f32) + r1[par, k, at, :].astype(f32)).astype(jnp.bfloat16)
             by_rows(add)
             message(R3, c, k).start()
+
+        def keep(k, p1, p2, st1, st2, s):
+            message(R2, c, k).wait_send()
             arrived(R2, c, k)
 
-            def keep(i):
+            def add(i):
                 at = pl.ds(i, sub)
                 t = term[par, k, pl.ds(pl.multiple_of(p1 * block + i, sub), sub), :]
-                run[sl, k, at, :] = t.astype(f32) + r2[par, k, at, :].astype(f32)
-            by_rows(keep)
-        colours(body)
+                run[par, k, at, :] = t.astype(f32) + r2[par, k, at, :].astype(f32)
+            by_rows(add)
+        colours(pass_on)
+        colours(keep)
 
     def stage2(c):
-        par, sl = c % 2, c % 3
+        par = c % 2
 
         def body(k, p1, p2, st1, st2, s):
             message(R3, c, k).wait_send()
@@ -153,68 +157,77 @@
 
             def add(i):
                 at = pl.ds(i, sub)
-                run[sl, k, at, :] = run[sl, k, at, :] + r3[par, k, at, :].astype(f32)
+                run[par, k, at, :] = run[par, k, at, :] + r3[par, k, at, :].astype(f32)
             by_rows(add)
-            s1[par, k] = run[sl, k, rows_of(wrap(p2, 2) * sub, sub), :].astype(jnp.bfloat16)
-            s2[par, k] = run[sl, k, rows_of(wrap(p2, s) * sub, sub), :].astype(jnp.bfloat16)
+            s1[par, k] = run[par, k, rows_of(wrap(p2, 2) * sub, sub), :].astype(jnp.bfloat16)
+            s2[par, k] = run[par, k, rows_of(wrap(p2, s) * sub, sub), :].astype(jnp.bfloat16)
             message(Q1, c, k).start()
             message(Q2, c, k).start()
         colours(body)
 
     def stage3(c):
-        par, sl = c % 2, c % 3
-
-        def body(k, p1, p2, st1, st2, s):
+        par = c % 2
+
+        def pass_on(k, p1, p2, st1, st2, s):
             message(Q1, c, k).wait_send()
-            message(Q2, c, k).wait_send()
             arrived(Q1, c, k)
-            there = run[sl, k, rows_of(wrap(p2, -s) * sub, sub), :]
+            there = run[par, k, rows_of(wrap(p2, -s) * sub, sub), :]
             cq[par, k] = (there + q1[par, k].astype(f32)).astype(jnp.bfloat16)
             message(Q3, c, k).start()
+
+        def keep(k, p1, p2, st1, st2, s):
+            message(Q2, c, k).wait_send()
             arrived(Q2, c, k)
             mine = rows_of(p2 * sub, sub)
-            run[sl, k, mine, :] = run[sl, k, mine, :] + q2[par, k].astype(f32)
-        colours(body)
+            run[par, k, mine, :] = run[par, k, mine, :] + q2[par, k].astype(f32)
+        colours(pass_on)
+        colours(keep)
 
     def stage4(c):
-        par, sl = c % 2, c % 3
+        par = c % 2
 
         def body(k, p1, p2, st1, st2, s):
             message(Q3, c, k).wait_send()
             arrived(Q3, c, k)
             mine = rows_of(p2 * sub, sub)
-            fin[par, k] = (run[sl, k, mine, :] + q3[par, k].astype(f32)).astype(jnp.bfloat16)
+            fin[par, k] = (run[par, k, mine, :] + q3[par, k].astype(f32)).astype(jnp.bfloat16)
             message(G1, c, k).start()
-            message(G2, c, k).start()
             own_copy(c, k).start()
         colours(body)
+        colours(lambda k, *_: message(G2, c, k).start())
 
     def stage5(c):
-        def body(k, *_):
+        def pass_on(k, *_):
             message(G1, c, k).wait_send()
+            arrived(G1, c, k)
+            message(G3, c, k).start()
+
+        def rest(k, *_):
             message(G2, c, k).wait_send()
             own_copy(c, k).wait()
-            arrived(G1, c, k)
-            message(G3, c, k).start()
             arrived(G2, c, k)
-        colours(body)
+        colours(pass_on)
+        colours(rest)
 
     def stage6(c):
         def body(k, *_):
             message(G3, c, k).wait_send()
             arrived(G3, c, k)
             message(H1, c, k).start()
-            message(H2, c, k).start()
         colours(body)
+        colours(lambda k, *_: message(H2, c, k).start())
 
     def stage7(c):
-        def body(k, *_):
+        def pass_on(k, *_):
             message(H1, c, k).wait_send()
-            message(H2, c, k).wait_send()
             arrived(H1, c, k)
             message(H3, c, k).start()
+
+        def rest(k, *_):
+            message(H2, c, k).wait_send()
             arrived(H2, c, k)
-        colours(body)
+        colours(pass_on)
+        colours(rest)
 
     def stage8(c):
         def body(k, *_):
@@ -227,9 +240,9 @@
 
     def w_copies(g):
         at = pl.ds(pl.multiple_of((g % tiles) * tile, tile), tile)
-        slot = g % 2
-        return (pltpu.make_async_copy(wg_hbm.at[:, at], wgb.at[slot], wg_sem.at[slot]),
-                pltpu.make_async_copy(wu_hbm.at[:, at], wub.at[slot], wu_sem.at[slot]))
+        slot = g % SLOTS
+        return (pltpu.make_async_copy(wg_hbm.at[:, at], wb.at[slot, :, pl.ds(0, tile)], wg_sem.at[slot]),
+                pltpu.make_async_copy(wu_hbm.at[:, at], wb.at[slot, :, pl.ds(tile, tile)], wu_sem.at[slot]))
 
     def colour_at(j):
         return (j % 2) * 2 + j // 2
@@ -239,82 +252,104 @@
         return pltpu.make_async_copy(wd_hbm.at[:, at], wdb.at[j % 2], wd_sem.at[j % 2])
 
     x_copy(0).start()
-    for g in range(2):
+    for g in range(SLOTS):
         for copy in w_copies(g):
             copy.start()
-    for j in range(2):
-        d_copy(j).start()
-
-    def hidden(t):
-        x_copy(t).wait()
-
-        def one(n, carry):
-            g = t * tiles + n
-            slot = g % 2
-            for copy in w_copies(g):
-                copy.wait()
-            gate = jnp.dot(xb[...], wgb[slot], preferred_element_type=f32)
-            up = jnp.dot(xb[...], wub[slot], preferred_element_type=f32)
-            at = pl.ds(pl.multiple_of(n * tile, tile), tile)
-            hb[:, at] = (gate * jax.nn.sigmoid(gate) * up).astype(jnp.bfloat16)
-
-            @pl.when(g + 2 < chunks * tiles)
-            def _():
-                for copy in w_copies(g + 2):
-                    copy.start()
-            return carry
-        lax.fori_loop(0, tiles, one, 0)
-
-        @pl.when(t + 1 < chunks)
+
+    def hidden(t, n):
+        @pl.when(n == 0)
+        def _():
+            x_copy(t).wait()
+        g = t * tiles + n
+        slot = g % SLOTS
+        for copy in w_copies(g):
+            copy.wait()
+        both = jnp.dot(xb[...], wb[slot], preferred_element_type=f32)
+        gate, up = both[:, :tile], both[:, tile:]
+        at = pl.ds(pl.multiple_of(n * tile, tile), tile)
+        hb[:, at] = (gate * jax.nn.sigmoid(gate) * up).astype(jnp.bfloat16)
+
+        @pl.when(g + SLOTS < chunks * tiles)
+        def _():
+            for copy in w_copies(g + SLOTS):
+                copy.start()
+
+        @pl.when((t == 0) & (n >= tiles - 2))
+        def _():
+            d_copy(n - (tiles - 2)).start()
+
+        @pl.when((n == tiles - 1) & (t + 1 < chunks))
         def _():
             x_copy(t + 1).start()
 
-    def down(t):
-        def one(j, carry):
-            k = colour_at(j)
-            d_copy(j).wait()
-            term[t % 2, k] = jnp.dot(hb[...], wdb[j % 2], preferred_element_type=f32).astype(jnp.bfloat16)
-
-            @pl.when((j + 2 < COLOURS) | (t + 1 < chunks))
-            def _():
-                d_copy((j + 2) % COLOURS).start()
-            message(R1, t, k).start()
-            message(R2, t, k).start()
-            return carry
-        lax.fori_loop(0, COLOURS, one, 0)
-
-    late = (stage8, stage7, stage6, stage5, stage4, stage3, stage2)
-    steps = chunks + 8
-
-    def step(t, carry):
-        @pl.when(t > 0)
-        def _():
-            for d in range(len(neighbours)):
-                pl.semaphore_wait(credit.at[d], 1)
-
-        for i, stage in enumerate(late):
-            lag = 8 - i
-
+    def down(t, j):
+        k = colour_at(j)
+        d_copy(j).wait()
+        term[t % 2, k] = jnp.dot(hb[...], wdb[j % 2], preferred_element_type=f32).astype(jnp.bfloat16)
+        message(R1, t, k).start()
+        message(R2, t, k).start()
+
+        @pl.when((j + 2 < COLOURS) | (t + 1 < chunks))
+        def _():
+            d_copy((j + 2) % COLOURS).start()
+
+    steps = chunks + 6
+
+    def handle(t, *stages):
+        for lag, stage in stages:
             @pl.when((t >= lag) & (t < chunks + lag))
             def _(stage=stage, lag=lag):
                 stage(t - lag)
 
-        @pl.when(t < chunks)
-        def _():
-            hidden(t)
-
-        @pl.when((t >= 1) & (t < chunks + 1))
-        def _():
-            stage1(t - 1)
+    def at_tile(n, late):
+        return n == max(tiles - 1 - late, 0)
+
+    def step(t, carry):
+        @pl.when(t > 0)
+        def _():
+            for d in range(len(neighbours)):
+                pl.semaphore_wait(credit.at[d], 1)
+
+        handle(t, (5, stage7))
+
+        def tile_step(n, carry):
+            @pl.when(t < chunks)
+            def _():
+                hidden(t, n)
+
+            @pl.when(at_tile(n, 4))
+            def _():
+                handle(t, (6, stage8), (3, stage5))
+
+            @pl.when(at_tile(n, 2))
+            def _():
+                handle(t, (2, stage3))
+
+            @pl.when(at_tile(n, 1))
+            def _():
+                handle(t, (4, stage6), (1, stage1))
+            return carry
+        lax.fori_loop(0, tiles, tile_step, 0)
 
         @pl.when(t < steps - 1)
         def _():
             for d, other in enumerate(neighbours):
                 pl.semaphore_signal(credit.at[d], inc=1, device_id=dev(other), device_id_type=MESH)
 
-        @pl.when(t < chunks)
-        def _():
-            down(t)
+        def colour_step(j, carry):
+            @pl.when(j == 1)
+            def _():
+                handle(t, (2, stage4))
+
+            @pl.when(j == 2)
+            def _():
+                handle(t, (1, stage2))
+
+            @pl.when(t < chunks)
+            def _():
+                down(t, j)
+            return carry
+        lax.fori_loop(0, COLOURS, colour_step, 0)
         return carry
 
     lax.fori_loop(0, steps, step, 0)
@@ -342,14 +377,14 @@
             out_specs=any_spec,
             scratch_shapes=[
                 pltpu.VMEM((m, d), bf16),
-                pltpu.VMEM((2, d, tile), bf16), pltpu.VMEM((2, d, tile), bf16),
+                pltpu.VMEM((SLOTS, d, 2 * tile), bf16),
                 pltpu.VMEM((2, ff, q), bf16),
                 pltpu.VMEM((m, ff), bf16),
                 pltpu.VMEM((2, COLOURS, m, q), bf16),
                 big, big, big, big,
-                pltpu.VMEM((3, COLOURS, block, q), jnp.float32),
+                pltpu.VMEM((2, COLOURS, block, q), jnp.float32),
                 small, small, small, small, small, small, small,
-                dma, dma((2,)), dma((2,)), dma((2,)), dma((2, COLOURS)),
+                dma, dma((SLOTS,)), dma((SLOTS,)), dma((2,)), dma((2, COLOURS)),
                 dma((12, 2, COLOURS)), dma((12, 2, COLOURS)),
                 pltpu.SemaphoreType.REGULAR((4,)),
             ],

time: 364 us -> 355 us (0.975)
  Pallas kernels: 343 us -> 335 us
    pallas_call x1, Pallas kernels: 343 us -> 335 us  [body(): pl.pallas_call(functools.partial(kernel, (side, chunks, m, q, tiles, tile...]
where the time goes in v2:
time: 355 us
  Pallas kernels  335 us (94%)
  local copies, waits for them, and re-layouts  20.2 us (6%)
    pallas_call x1, Pallas kernels, body(): pl.pallas_call(functools.partial(kernel, (side, chunks, m, q, tiles, tile...  335 us
    unnamed x1, local copies, waits for them, and re-layouts  20.2 us

profile of v2, /device:TPU:97, one launch (start us, length us, event | category | flops | bytes accessed | tf_op | source)
XLA Modules:
  0.0 355.4 jit_solution(8798576304859146136)
XLA Ops:
  0.0 335.2 %shard_map.46 = bf16[2048,7168]{1,0:T(8,128)(2,1)} custom-call(bf16[2048,7168]{1,0:T(8,128)(2,1)} %x_hbm.1, bf16[7168,1280]{1,0:T(8,128)(2,1)} %wg_hbm.1, bf16[7168,1280]{1,0:T(8,128)(2,1)} %wu_hbm.1, bf16[1280,7168]{1,0:T(8,128)(2,1)} %wd_hbm.1), custom_call_target="tpu_custom_call" | custom-call | tf_op jit(solution)/shard_map/pallas_call | solution.py:373
  335.2 20.2 %copy.6 = bf16[2048,7168]{1,0:T(8,128)(2,1)} copy(bf16[2048,7168]{1,0:T(8,128)(2,1)} %shard_map.46) | data formatting | bytes 58720256

commit v3 on v2

--- a/solution.py
+++ b/solution.py
@@ -40,11 +40,6 @@
         return (p + delta + side) % side
 
     neighbours = [step_on(px, side, 1), step_on(px, side, -1), step_on(py, 1, 1), step_on(py, 1, -1)]
-    barrier = pltpu.get_barrier_semaphore()
-    for other in neighbours:
-        pl.semaphore_signal(barrier, inc=1, device_id=dev(other), device_id_type=MESH)
-    pl.semaphore_wait(barrier, len(neighbours))
-
     def remote(kind, c, k, src, dst, to):
         return pltpu.make_async_remote_copy(
             src_ref=src, dst_ref=dst, send_sem=send_sem.at[kind, c % 2, k],
@@ -256,6 +251,11 @@
         for copy in w_copies(g):
             copy.start()
 
+    barrier = pltpu.get_barrier_semaphore()
+    for other in neighbours:
+        pl.semaphore_signal(barrier, inc=1, device_id=dev(other), device_id_type=MESH)
+    pl.semaphore_wait(barrier, len(neighbours))
+
     def hidden(t, n):
         @pl.when(n == 0)
         def _():
@@ -293,7 +293,7 @@
         def _():
             d_copy((j + 2) % COLOURS).start()
 
-    steps = chunks + 6
+    steps = chunks + 5
 
     def handle(t, *stages):
         for lag, stage in stages:
@@ -310,8 +310,6 @@
             for d in range(len(neighbours)):
                 pl.semaphore_wait(credit.at[d], 1)
 
-        handle(t, (5, stage7))
-
         def tile_step(n, carry):
             @pl.when(t < chunks)
             def _():
@@ -319,15 +317,19 @@
 
             @pl.when(at_tile(n, 4))
             def _():
-                handle(t, (6, stage8), (3, stage5))
+                handle(t, (5, stage7))
+
+            @pl.when(at_tile(n, 3))
+            def _():
+                handle(t, (2, stage3), (3, stage5))
 
             @pl.when(at_tile(n, 2))
             def _():
-                handle(t, (2, stage3))
+                handle(t, (1, stage1), (4, stage6))
 
             @pl.when(at_tile(n, 1))
             def _():
-                handle(t, (4, stage6), (1, stage1))
+                handle(t, (2, stage4), (5, stage8))
             return carry
         lax.fori_loop(0, tiles, tile_step, 0)
 
@@ -336,15 +338,9 @@
             for d, other in enumerate(neighbours):
                 pl.semaphore_signal(credit.at[d], inc=1, device_id=dev(other), device_id_type=MESH)
 
+        handle(t, (1, stage2))
+
         def colour_step(j, carry):
-            @pl.when(j == 1)
-            def _():
-                handle(t, (2, stage4))
-
-            @pl.when(j == 2)
-            def _():
-                handle(t, (1, stage2))
-
             @pl.when(t < chunks)
             def _():
                 down(t, j)

time: 355 us -> 353 us (level)
  no operation moved by 1% of the time
where the time goes in v3:
time: 353 us; the launch traced here: 352 us
  Pallas kernels  332 us (94%)
  local copies, waits for them, and re-layouts  20.2 us (6%)
    pallas_call x1, Pallas kernels, body(): pl.pallas_call(functools.partial(kernel, (side, chunks, m, q, tiles, tile...  332 us
    unnamed x1, local copies, waits for them, and re-layouts  20.2 us

profile of v3, /device:TPU:97, one launch (start us, length us, event | category | flops | bytes accessed | tf_op | source)
XLA Modules:
  0.0 352.0 jit_solution(6803285444444301027)
XLA Ops:
  0.0 331.8 %shard_map.46 = bf16[2048,7168]{1,0:T(8,128)(2,1)} custom-call(bf16[2048,7168]{1,0:T(8,128)(2,1)} %x_hbm.1, bf16[7168,1280]{1,0:T(8,128)(2,1)} %wg_hbm.1, bf16[7168,1280]{1,0:T(8,128)(2,1)} %wu_hbm.1, bf16[1280,7168]{1,0:T(8,128)(2,1)} %wd_hbm.1), custom_call_target="tpu_custom_call" | custom-call | tf_op jit(solution)/shard_map/pallas_call | solution.py:369
  331.8 20.2 %copy.6 = bf16[2048,7168]{1,0:T(8,128)(2,1)} copy(bf16[2048,7168]{1,0:T(8,128)(2,1)} %shard_map.46) | data formatting | bytes 58720256
